TPU v7x, 32 devices: a whole 2x2x4 slice. The times are simulated.
32 devices in a mesh: grp: 2 (over y), sp: 16 (over z, x, core).
Axes of the slice: x: 2, y: 2, z: 4, core: 2. Of those that a mesh axis runs over, the one named last changes fastest.
Arguments:
- alpha: float32 [20, 16, 4096], P('grp', None, 'sp'), may hold values from -6 to 6
- ensemble: bfloat16 [20, 3, 16, 4096], P('grp', None, None, 'sp'), may hold values from -6 to 6
- static_std: float32 [3, 16, 4096], P(None, 'grp', 'sp'), may hold values from 0.2 to 1
- control: float32 [3, 16, 4096], P(None, 'grp', 'sp'), may hold values from -6 to 6
- loc_spectrum: float32 [1024], replicated, may hold values from 0.00024414062 to 0.001953125
- obs_cell: int32 [32768], P(('grp', 'sp')), may hold values from 0 to 65535, as said below
- obs_step: int32 [32768], P(('grp', 'sp')), may hold values from 0 to 2
- innovation: float32 [32768], P(('grp', 'sp')), may hold values from -6 to 6
- obs_weight: float32 [32768], P(('grp', 'sp')), may hold values from 0.5 to 4
Outputs:
- grad_alpha: float32 [20, 16, 4096], P('grp', None, 'sp')
- grad_control: float32 [3, 16, 4096], P(None, 'grp', 'sp')
Inputs may be any that keep to these rules, and one draw needn't show every extreme that they name: `obs_cell`: an entry is row * 4096 + column. Entries 1024 * b to 1024 * (b + 1) - 1 lie in the tile of 8 rows from row 8 * (b // 16) and 256 columns from column 256 * (b % 16).
All inputs are finite; a program needn't handle non-finite values.
Results may differ from a plain program's by a relative error of at most 0.0075.
Values may be sent and summed in bfloat16 or wider, within the bound.
A program may use at most 128 MiB of HBM per device.

v0:
```python
import math
import jax
import jax.numpy as jnp
import numpy as np
from jax import lax
from jax.sharding import PartitionSpec as P

COURANT = 0.4


def tables(parts, cols, waves):
    length = parts * cols
    inner_waves = waves // parts
    k1 = np.arange(parts)
    turn = 2 * np.pi * (np.outer(k1, np.arange(parts)) % parts) / parts
    outer = np.concatenate([np.cos(turn), -np.sin(turn)])
    twist = 2 * np.pi * np.outer(k1, np.arange(cols)) / length
    phase = 2 * np.pi * (np.outer(np.arange(cols), np.arange(inner_waves)) % cols) / cols
    c, s = (np.cos(phase), np.sin(phase))
    inner = np.block([[c, -s], [s, c]])
    return [np.asarray(t, np.float32) for t in (outer, np.cos(twist), np.sin(twist), inner)]


def mul(a, b):
    return jnp.dot(a, b, precision=lax.Precision.HIGH, preferred_element_type=jnp.float32)


def spectral_filter(blocks, loc_spectrum):
    parts, items, cols = blocks.shape
    outer, tw_c, tw_s, inner = tables(parts, cols, loc_spectrum.shape[0])
    tw_c, tw_s = (tw_c[:, None, :], tw_s[:, None, :])
    half = inner.shape[1] // 2
    weights = loc_spectrum.reshape(half, parts).T
    weights = jnp.concatenate([weights, weights], axis=1)[:, None, :]
    big = np.kron(outer, np.eye(items, dtype=np.float32))
    y = mul(big, blocks.astype(jnp.float32).reshape(parts * items, cols))
    y = y.reshape(2, parts, items, cols)
    y = jnp.concatenate([y[0] * tw_c + y[1] * tw_s, y[1] * tw_c - y[0] * tw_s], axis=2)
    z = mul(y.reshape(parts * items, 2 * cols), inner)
    z = (z.reshape(parts, items, 2 * half) * weights).reshape(parts * items, 2 * half)
    v = mul(z, inner.T).reshape(parts, items, 2, cols)
    re, im = (v[:, :, 0], v[:, :, 1])
    v = jnp.stack([re * tw_c - im * tw_s, im * tw_c + re * tw_s])
    return mul(big.T, v.reshape(2 * parts * items, cols)).reshape(parts, items, cols)


def dx(q):
    return 0.5 * (jnp.roll(q, -1, axis=-1) - jnp.roll(q, 1, axis=-1))


def dy(q):
    padded = jnp.pad(q, ((1, 1), (0, 0)))
    return 0.5 * (padded[2:] - padded[:-2])


def model_step(state, rotation):
    h, u, w = state
    h = h - COURANT * (dx(u) + dy(w))
    return (h, u - COURANT * dx(h) + rotation * w, w - COURANT * dy(h) - rotation * u)


def adjoint_step(state, rotation):
    h, u, w = state
    a = h + COURANT * (dx(u) + dy(w))
    return (a, u - rotation * w + COURANT * dx(a), w + rotation * u + COURANT * dy(a))


HALO = 8


def widen(block):
    count = lax.axis_size("sp")
    up = [(i, (i + 1) % count) for i in range(count)]
    down = [(b, a) for a, b in up]
    low = lax.ppermute(block[..., -HALO:], "sp", up)
    high = lax.ppermute(block[..., :HALO], "sp", down)
    return jnp.concatenate([low, block, high], axis=-1)


def split2(x):
    hi = x.astype(jnp.bfloat16)
    return (hi, (x - hi.astype(jnp.float32)).astype(jnp.bfloat16))


def per_device(
    alpha, ensemble, static_std, control, loc_spectrum, obs_cell, obs_step, innovation, obs_weight
):
    members, rows, cols = alpha.shape
    groups, parts = (lax.axis_size("grp"), lax.axis_size("sp"))
    spread = 1.0 / math.sqrt(members * groups - 1)
    tile_rows = control.shape[1]
    own = rows // parts
    first_row = lax.axis_index("grp") * tile_rows
    first_col = lax.axis_index("sp") * cols

    def localize(fields):
        sent = fields.astype(jnp.bfloat16).transpose(1, 0, 2)
        got = lax.all_to_all(sent, "sp", 0, 0, tiled=True)
        out = spectral_filter(got.reshape(parts, own * members, cols), loc_spectrum)
        out = out.astype(jnp.bfloat16).reshape(rows, members, cols)
        return lax.all_to_all(out, "sp", 0, 0, tiled=True).transpose(1, 0, 2)

    localized = localize(alpha).astype(jnp.float32)
    partial = jnp.sum(ensemble.astype(jnp.float32) * localized[:, None], axis=0)
    base = jnp.zeros((3, rows, cols), jnp.float32)
    base = lax.dynamic_update_slice(base, static_std * control, (0, first_row, 0))
    increment = lax.psum(base + spread * partial, "grp")
    rotation = (0.1 + 0.2 * (jnp.arange(rows, dtype=jnp.float32) + 0.5) / rows)[:, None]
    state0 = tuple(widen(increment))
    state1 = model_step(state0, rotation)
    state2 = model_step(state1, rotation)
    heights = jnp.stack([s[0] for s in (state0, state1, state2)])[..., HALO:-HALO]
    heights = lax.dynamic_slice_in_dim(heights, first_row, tile_rows, axis=1)
    heights = heights.reshape(3 * tile_rows, cols)
    row = obs_cell // (cols * parts) - first_row
    col = obs_cell % (cols * parts) - first_col
    in_col = (col[:, None] == jnp.arange(cols)).astype(jnp.bfloat16)
    in_row = (obs_step * tile_rows + row)[:, None] == jnp.arange(3 * tile_rows)
    picked = jnp.dot(in_col, jnp.concatenate(split2(heights)).T, preferred_element_type=jnp.float32)
    picked = picked[:, : 3 * tile_rows] + picked[:, 3 * tile_rows :]
    observed = jnp.sum(jnp.where(in_row, picked, 0.0), axis=1)
    misfit = obs_weight * (observed - innovation)
    placed = jnp.where(in_row, misfit[:, None], 0.0)
    forcing = jnp.dot(
        jnp.concatenate(split2(placed), axis=1).T, in_col, preferred_element_type=jnp.float32
    )
    forcing = (forcing[: 3 * tile_rows] + forcing[3 * tile_rows :]).reshape(3, tile_rows, cols)
    forcing = widen(lax.all_gather(forcing, "grp", axis=1, tiled=True))
    zero = jnp.zeros_like(forcing[0])
    h, u, w = adjoint_step((forcing[2], zero, zero), rotation)
    h, u, w = adjoint_step((h + forcing[1], u, w), rotation)
    adjoint = jnp.stack([h + forcing[0], u, w])[..., HALO:-HALO]
    tile = lax.dynamic_slice_in_dim(adjoint, first_row, tile_rows, axis=1)
    grad_control = control + static_std * tile
    half = adjoint.astype(jnp.bfloat16).astype(jnp.float32)
    weighted = jnp.sum(ensemble.astype(jnp.float32) * half[None], axis=1)
    grad_alpha = alpha + spread * localize(weighted).astype(jnp.float32)
    return (grad_alpha, grad_control)


def solution(mesh):
    flat = P(("grp", "sp"))
    tile = P(None, "grp", "sp")
    return jax.shard_map(
        per_device,
        mesh=mesh,
        in_specs=(
            P("grp", None, "sp"),
            P("grp", None, None, "sp"),
            tile,
            tile,
            P(),
            flat,
            flat,
            flat,
            flat,
        ),
        out_specs=(P("grp", None, "sp"), tile),
        check_vma=False,
    )
```

profile of v0, /device:TPU:0, one launch (start us, length us, event | category | flops | bytes accessed | tf_op | source)
XLA Modules:
  0.0 93.3 jit_solution(1954184808317779153)
XLA Ops:
  0.6 0.9 convert_bitcast_fusion.2
  1.6 0.7 copy.66
  2.3 7.5 %all-to-all-start = ((bf16[16,10,256]{2,1,0:T(8,128)(2,1)}), bf16[16,10,256]{2,1,0:T(8,128)(2,1)S(1)}, u32[]{:S(2)}, u32[]{:S(2)}) async-start(bf16[16,10,256]{2,1,0:T(8,128)(2,1)} %copy.66), calls=%async_computation | async-start | bytes 262144 | tf_op jit(solution)/shard_map/all_to_all | solution.py:98
  9.8 0.7 copy-done.7
  10.6 0.7 copy-done.8
  11.3 0.6 copy-done.13
  12.2 5.5 %all-to-all-done = bf16[16,10,256]{2,1,0:T(8,128)(2,1)S(1)} async-done(((bf16[16,10,256]{2,1,0:T(8,128)(2,1)}), bf16[16,10,256]{2,1,0:T(8,128)(2,1)S(1)}, u32[]{:S(2)}, u32[]{:S(2)}) %all-to-all-start) | async-done | bytes 81952 | tf_op jit(solution)/shard_map/all_to_all | solution.py:98
  17.7 0.2 fusion.94
  18.1 0.9 copy-done.1
  19.0 0.4 fusion
  19.4 0.6 copy-done.6
  20.0 0.3 fusion.23
  20.4 0.2 copy.71
  20.6 0.9 copy-done.3
  21.5 0.3 fusion.1
  21.8 0.7 convert_element_type.81
  22.5 3.5 %all-to-all-start.1 = ((bf16[16,10,256]{2,1,0:T(8,128)(2,1)}), bf16[16,10,256]{2,1,0:T(8,128)(2,1)S(1)}, u32[]{:S(2)}, u32[]{:S(2)}) async-start(bf16[16,10,256]{2,1,0:T(8,128)(2,1)} %convert_element_type.81), calls=%async_computation.1 | async-start | bytes 262144 | tf_op jit(solution)/shard_map/all_to_all | solution.py:101
  26.0 7.8 %all-to-all-done.1 = bf16[16,10,256]{2,1,0:T(8,128)(2,1)S(1)} async-done(((bf16[16,10,256]{2,1,0:T(8,128)(2,1)}), bf16[16,10,256]{2,1,0:T(8,128)(2,1)S(1)}, u32[]{:S(2)}, u32[]{:S(2)}) %all-to-all-start.1) | async-done | bytes 81952 | tf_op jit(solution)/shard_map/all_to_all | solution.py:101
  33.9 0.1 copy.72
  34.0 0.8 copy-done.2
  34.9 0.7 copy-done.9
  35.7 8.6 %psum.7 = f32[3,16,256]{2,1,0:T(8,128)S(1)} all-reduce(f32[3,16,256]{2,1,0:T(8,128)S(1)} %add_dynamic-update-slice_fusion), channel_id=1, replica_groups=mesh['grp'=2,'sp'=16] {'grp'}, use_global_device_ids=true, to_apply=%region_1.0 | all-reduce | flops 12288 | bytes 98304 | tf_op jit(solution)/shard_map/psum | solution.py:107
  44.4 4.4 %collective-permute-start.1 = (f32[3,16,8]{2,1,0:T(8,128)S(1)}, f32[3,16,8]{2,1,0:T(8,128)S(1)}, u32[]{:S(2)}, u32[]{:S(2)}) collective-permute-start(f32[3,16,8]{2,1,0:T(8,128)S(1)} %get-tuple-element.34), channel_id=1, source_target_pairs={{1,0},{2,1},{3,2},{4,3},{5,4},{6,5},{7,6},{8,7},{9,8},{10,9},{11,1... | collective-permute-start | bytes 4616 | tf_op jit(solution)/shard_map/ppermute | solution.py:76
  48.9 1.5 %collective-permute-done = f32[3,16,8]{2,1,0:T(8,128)S(1)} collective-permute-done((f32[3,16,8]{2,1,0:T(8,128)S(1)}, f32[3,16,8]{2,1,0:T(8,128)S(1)}, u32[]{:S(2)}, u32[]{:S(2)}) %collective-permute-start) | collective-permute-done | bytes 1568 | tf_op jit(solution)/shard_map/ppermute | solution.py:75
  50.4 0.1 pad_maximum_fusion.2
  50.9 0.1 fusion.60
  51.3 0.4 fusion.4
  51.7 0.6 copy-done.14
  52.4 0.4 fusion.3
  52.8 4.5 %all_gather.3 = f32[3,16,256]{2,1,0:T(8,128)S(1)} all-gather(f32[3,8,256]{2,1,0:T(8,128)S(1)} %fusion.57), channel_id=1, replica_groups=mesh['grp'=2,'sp'=16] {'grp'}, dimensions={1}, use_global_device_ids=true | all-gather | bytes 73728 | tf_op jit(solution)/shard_map/all_gather | solution.py:128
  57.3 4.4 %collective-permute-start.3 = (f32[3,16,8]{2,1,0:T(8,128)S(1)}, f32[3,16,8]{2,1,0:T(8,128)S(1)}, u32[]{:S(2)}, u32[]{:S(2)}) collective-permute-start(f32[3,16,8]{2,1,0:T(8,128)S(1)} %get-tuple-element.32), channel_id=1, source_target_pairs={{1,0},{2,1},{3,2},{4,3},{5,4},{6,5},{7,6},{8,7},{9,8},{10,9},{11,1... | collective-permute-start | bytes 4616 | tf_op jit(solution)/shard_map/ppermute | solution.py:76
  61.9 1.4 %collective-permute-done.2 = f32[3,16,8]{2,1,0:T(8,128)S(1)} collective-permute-done((f32[3,16,8]{2,1,0:T(8,128)S(1)}, f32[3,16,8]{2,1,0:T(8,128)S(1)}, u32[]{:S(2)}, u32[]{:S(2)}) %collective-permute-start.2) | collective-permute-done | bytes 1568 | tf_op jit(solution)/shard_map/ppermute | solution.py:75
  63.3 0.1 pad_maximum_fusion.3
  63.6 0.1 fusion.41
  64.1 0.1 fusion.68
  64.4 13.5 %all_to_all.20 = bf16[16,10,256]{2,1,0:T(8,128)(2,1)S(1)} all-to-all(bf16[16,10,256]{2,1,0:T(8,128)(2,1)S(1)} %copy.73), channel_id=1, replica_groups=mesh['grp'=2,'sp'=16] {'sp'}, dimensions={0} | all-to-all | bytes 163840 | tf_op jit(solution)/shard_map/all_to_all | solution.py:98
  77.9 0.2 fusion.95
  78.3 0.4 convolution_multiply_fusion
  78.7 0.5 copy-done.5
  79.2 0.3 fusion.21
  79.6 0.2 copy.77
  79.9 0.3 fusion.2
  80.2 0.7 convert_element_type.96
  80.9 3.6 %all-to-all-start.3 = ((bf16[16,10,256]{2,1,0:T(8,128)(2,1)}), bf16[16,10,256]{2,1,0:T(8,128)(2,1)S(1)}, u32[]{:S(2)}, u32[]{:S(2)}) async-start(bf16[16,10,256]{2,1,0:T(8,128)(2,1)} %convert_element_type.96), calls=%async_computation.3 | async-start | bytes 262144 | tf_op jit(solution)/shard_map/all_to_all | solution.py:101
  84.5 0.6 multiply_add_fusion.4
  85.1 7.2 %all-to-all-done.3 = bf16[16,10,256]{2,1,0:T(8,128)(2,1)S(1)} async-done(((bf16[16,10,256]{2,1,0:T(8,128)(2,1)}), bf16[16,10,256]{2,1,0:T(8,128)(2,1)S(1)}, u32[]{:S(2)}, u32[]{:S(2)}) %all-to-all-start.3) | async-done | bytes 81952 | tf_op jit(solution)/shard_map/all_to_all | solution.py:101
  92.4 0.1 bitcast_add_fusion
  92.5 0.8 copy.79
  (87 shorter events, 2.8 us)
Async XLA Ops:
  2.2 7.5 %copy-start.11 = (s32[1024]{0:T(1024)S(1)}, s32[1024]{0:T(1024)}, u32[]{:S(2)}) copy-start(s32[1024]{0:T(1024)} %param.27) | copy-start | bytes 12292
  2.2 7.6 %copy-start.12 = (s32[1024]{0:T(1024)S(1)}, s32[1024]{0:T(1024)}, u32[]{:S(2)}) copy-start(s32[1024]{0:T(1024)} %param.26) | copy-start | bytes 12292
  2.3 15.4 %all-to-all-start = ((bf16[16,10,256]{2,1,0:T(8,128)(2,1)}), bf16[16,10,256]{2,1,0:T(8,128)(2,1)S(1)}, u32[]{:S(2)}, u32[]{:S(2)}) async-start(bf16[16,10,256]{2,1,0:T(8,128)(2,1)} %copy.66), calls=%async_computation | async-start | bytes 262144 | tf_op jit(solution)/shard_map/all_to_all | solution.py:98
  9.8 0.7 copy-start.7
  10.5 0.7 copy-start.8
  11.3 0.7 copy-start.13
  11.3 6.4 %copy-start = (f32[320,160]{1,0:T(8,128)S(1)}, f32[320,160]{1,0:T(8,128)}, u32[]{:S(2)}) copy-start(f32[320,160]{1,0:T(8,128)} %constant.90.clone) | copy-start | bytes 614404
  18.1 1.0 %copy-start.1 = (f32[512,128,1]{1,0,2:T(8,128)S(1)}, f32[512,128,1]{1,0,2:T(8,128)}, u32[]{:S(2)}) copy-start(f32[512,128,1]{1,0,2:T(8,128)} %constant.116) | copy-start | bytes 786436
  19.0 0.9 %copy-start.6 = (f32[2,256,128,1]{2,1,0,3:T(8,128)S(1)}, f32[2,256,128,1]{2,1,0,3:T(8,128)}, u32[]{:S(2)}) copy-start(f32[2,256,128,1]{2,1,0,3:T(8,128)} %constant.117) | copy-start | bytes 786436
  20.6 0.9 %copy-start.3 = (f32[160,320]{1,0:T(8,128)S(1)}, f32[160,320]{1,0:T(8,128)}, u32[]{:S(2)}) copy-start(f32[160,320]{1,0:T(8,128)} %constant.95.clone) | copy-start | bytes 614404
  22.5 11.4 %all-to-all-start.1 = ((bf16[16,10,256]{2,1,0:T(8,128)(2,1)}), bf16[16,10,256]{2,1,0:T(8,128)(2,1)S(1)}, u32[]{:S(2)}, u32[]{:S(2)}) async-start(bf16[16,10,256]{2,1,0:T(8,128)(2,1)} %convert_element_type.81), calls=%async_computation.1 | async-start | bytes 262144 | tf_op jit(solution)/shard_map/all_to_all | solution.py:101
  33.9 0.9 %copy-start.2 = (bf16[10,3,16,256]{3,2,1,0:T(8,128)(2,1)S(1)}, bf16[10,3,16,256]{3,2,1,0:T(8,128)(2,1)}, u32[]{:S(2)}) copy-start(bf16[10,3,16,256]{3,2,1,0:T(8,128)(2,1)} %param.22) | copy-start | bytes 737284
  34.9 0.7 copy-start.9
  34.9 0.7 copy-start.10
  44.4 6.0 %collective-permute-start = (f32[3,16,8]{2,1,0:T(8,128)S(1)}, f32[3,16,8]{2,1,0:T(8,128)S(1)}, u32[]{:S(2)}, u32[]{:S(2)}) collective-permute-start(f32[3,16,8]{2,1,0:T(8,128)S(1)} %get-tuple-element.33), channel_id=1, source_target_pairs={{0,1},{1,2},{2,3},{3,4},{4,5},{5,6},{6,7},{7,8},{8,9},{9,10},{10,1... | collective-permute-start | bytes 4616 | tf_op jit(solution)/shard_map/ppermute | solution.py:75
  44.4 6.0 %collective-permute-start.1 = (f32[3,16,8]{2,1,0:T(8,128)S(1)}, f32[3,16,8]{2,1,0:T(8,128)S(1)}, u32[]{:S(2)}, u32[]{:S(2)}) collective-permute-start(f32[3,16,8]{2,1,0:T(8,128)S(1)} %get-tuple-element.34), channel_id=1, source_target_pairs={{1,0},{2,1},{3,2},{4,3},{5,4},{6,5},{7,6},{8,7},{9,8},{10,9},{11,1... | collective-permute-start | bytes 4616 | tf_op jit(solution)/shard_map/ppermute | solution.py:76
  51.6 0.7 copy-start.14
  51.6 0.7 copy-start.15
  57.3 6.0 %collective-permute-start.2 = (f32[3,16,8]{2,1,0:T(8,128)S(1)}, f32[3,16,8]{2,1,0:T(8,128)S(1)}, u32[]{:S(2)}, u32[]{:S(2)}) collective-permute-start(f32[3,16,8]{2,1,0:T(8,128)S(1)} %get-tuple-element.31), channel_id=1, source_target_pairs={{0,1},{1,2},{2,3},{3,4},{4,5},{5,6},{6,7},{7,8},{8,9},{9,10},{10,1... | collective-permute-start | bytes 4616 | tf_op jit(solution)/shard_map/ppermute | solution.py:75
  57.3 6.0 %collective-permute-start.3 = (f32[3,16,8]{2,1,0:T(8,128)S(1)}, f32[3,16,8]{2,1,0:T(8,128)S(1)}, u32[]{:S(2)}, u32[]{:S(2)}) collective-permute-start(f32[3,16,8]{2,1,0:T(8,128)S(1)} %get-tuple-element.32), channel_id=1, source_target_pairs={{1,0},{2,1},{3,2},{4,3},{5,4},{6,5},{7,6},{8,7},{9,8},{10,9},{11,1... | collective-permute-start | bytes 4616 | tf_op jit(solution)/shard_map/ppermute | solution.py:76
  78.3 1.0 %copy-start.5 = (f32[2,256,128,1]{2,1,3,0:T(8,128)S(1)}, f32[2,256,128,1]{2,1,3,0:T(8,128)}, u32[]{:S(2)}) copy-start(f32[2,256,128,1]{2,1,3,0:T(8,128)} %constant.118) | copy-start | bytes 786436
  80.9 11.5 %copy-start.4 = (f32[10,16,256]{2,1,0:T(8,128)S(1)}, f32[10,16,256]{2,1,0:T(8,128)}, u32[]{:S(2)}) copy-start(f32[10,16,256]{2,1,0:T(8,128)} %param.21) | copy-start | bytes 491524
  80.9 11.5 %all-to-all-start.3 = ((bf16[16,10,256]{2,1,0:T(8,128)(2,1)}), bf16[16,10,256]{2,1,0:T(8,128)(2,1)S(1)}, u32[]{:S(2)}, u32[]{:S(2)}) async-start(bf16[16,10,256]{2,1,0:T(8,128)(2,1)} %convert_element_type.96), calls=%async_computation.3 | async-start | bytes 262144 | tf_op jit(solution)/shard_map/all_to_all | solution.py:101
where the time goes:
time: 94.1 us; the launch traced here: 93.3 us
  blocking collectives  26.7 us (28%)
  starting transfers between devices  23.6 us (25%)
  waiting for transfers between devices  23.5 us (25%)
  local copies, waits for them, and re-layouts  12 us (13%)
  other arithmetic  3.23 us (3%)
  matrix products  3.1 us (3%)
  between operations  1.17 us (1%)
    all_to_all x2, waiting for transfers between devices, localize(): return lax.all_to_all(out, 'sp', 0, 0, tiled=True).transpose(1, 0, 2)  15.1 us
    all_to_all x1, blocking collectives, localize(): got = lax.all_to_all(sent, 'sp', 0, 0, tiled=True)  13.5 us
    ppermute x2, starting transfers between devices, widen(): high = lax.ppermute(block[..., :HALO], 'sp', down)  8.88 us
    psum x1, blocking collectives, per_device(): increment = lax.psum(base + spread * partial, 'grp')  8.65 us
    unnamed x33, local copies, waits for them, and re-layouts  7.9 us
    all_to_all x1, starting transfers between devices, localize(): got = lax.all_to_all(sent, 'sp', 0, 0, tiled=True)  7.52 us
    all_to_all x2, starting transfers between devices, localize(): return lax.all_to_all(out, 'sp', 0, 0, tiled=True).transpose(1, 0, 2)  7.16 us
    all_to_all x1, waiting for transfers between devices, localize(): got = lax.all_to_all(sent, 'sp', 0, 0, tiled=True)  5.51 us
  transfers between devices with their start and end apart: 7, of which 5 were waited for; matrix products, arithmetic and copies ran while one was open for 1% of the time, Pallas kernels for 0%

commit v1 on v0

--- a/solution.py
+++ b/solution.py
@@ -104,7 +104,7 @@
     partial = jnp.sum(ensemble.astype(jnp.float32) * localized[:, None], axis=0)
     base = jnp.zeros((3, rows, cols), jnp.float32)
     base = lax.dynamic_update_slice(base, static_std * control, (0, first_row, 0))
-    increment = lax.psum(base + spread * partial, "grp")
+    increment = jnp.sum(lax.all_gather(base + spread * partial, "grp"), axis=0)
     rotation = (0.1 + 0.2 * (jnp.arange(rows, dtype=jnp.float32) + 0.5) / rows)[:, None]
     state0 = tuple(widen(increment))
     state1 = model_step(state0, rotation)

time: 94.1 us -> 90.2 us (0.959)
  blocking collectives: 26.7 us -> 22.8 us
    psum x1 -> x0, blocking collectives: 8.65 us -> none  [per_device(): increment = lax.psum(base + spread * partial, 'grp')]
    all_gather x0 -> x1, blocking collectives: none -> 4.75 us  [per_device(): increment = jnp.sum(lax.all_gather(base + spread * partial, 'grp'), axis=0)]
where the time goes in v1:
time: 90.2 us; the launch traced here: 89.4 us
  starting transfers between devices  23.6 us (26%)
  waiting for transfers between devices  23.5 us (26%)
  blocking collectives  22.8 us (25%)
  local copies, waits for them, and re-layouts  12 us (13%)
  other arithmetic  3.25 us (4%)
  matrix products  3.09 us (3%)
  between operations  1.17 us (1%)
    all_to_all x2, waiting for transfers between devices, localize(): return lax.all_to_all(out, 'sp', 0, 0, tiled=True).transpose(1, 0, 2)  15.1 us
    all_to_all x1, blocking collectives, localize(): got = lax.all_to_all(sent, 'sp', 0, 0, tiled=True)  13.5 us
    ppermute x2, starting transfers between devices, widen(): high = lax.ppermute(block[..., :HALO], 'sp', down)  8.88 us
    unnamed x33, local copies, waits for them, and re-layouts  7.91 us
    all_to_all x1, starting transfers between devices, localize(): got = lax.all_to_all(sent, 'sp', 0, 0, tiled=True)  7.52 us
    all_to_all x2, starting transfers between devices, localize(): return lax.all_to_all(out, 'sp', 0, 0, tiled=True).transpose(1, 0, 2)  7.16 us
    all_to_all x1, waiting for transfers between devices, localize(): got = lax.all_to_all(sent, 'sp', 0, 0, tiled=True)  5.51 us
    all_gather x1, blocking collectives, per_device(): increment = jnp.sum(lax.all_gather(base + spread * partial, 'grp'), axis=0)  4.75 us
  transfers between devices with their start and end apart: 7, of which 5 were waited for; matrix products, arithmetic and copies ran while one was open for 1% of the time, Pallas kernels for 0%

profile of v1, /device:TPU:0, one launch (start us, length us, event | category | flops | bytes accessed | tf_op | source)
XLA Modules:
  0.0 89.4 jit_solution(6937438591136755106)
XLA Ops:
  0.6 0.9 %convert_bitcast_fusion.2 = bf16[16,10,256]{2,0,1:T(8,128)(2,1)S(1)} fusion(f32[10,16,256]{2,1,0:T(8,128)} %param.21), kind=kLoop, calls=%fused_computation.54 | loop fusion | flops 40960 | bytes 245760 | tf_op jit(solution)/shard_map/transpose | solution.py:97
  1.6 0.7 copy.66
  2.3 7.5 %all-to-all-start = ((bf16[16,10,256]{2,1,0:T(8,128)(2,1)}), bf16[16,10,256]{2,1,0:T(8,128)(2,1)S(1)}, u32[]{:S(2)}, u32[]{:S(2)}) async-start(bf16[16,10,256]{2,1,0:T(8,128)(2,1)} %copy.66), calls=%async_computation | async-start | bytes 262144 | tf_op jit(solution)/shard_map/all_to_all | solution.py:98
  9.8 0.7 copy-done.7
  10.6 0.7 copy-done.8
  11.3 0.6 copy-done.13
  12.2 5.5 %all-to-all-done = bf16[16,10,256]{2,1,0:T(8,128)(2,1)S(1)} async-done(((bf16[16,10,256]{2,1,0:T(8,128)(2,1)}), bf16[16,10,256]{2,1,0:T(8,128)(2,1)S(1)}, u32[]{:S(2)}, u32[]{:S(2)}) %all-to-all-start) | async-done | bytes 81952 | tf_op jit(solution)/shard_map/all_to_all | solution.py:98
  17.7 0.2 fusion.95
  18.1 0.9 %copy-done.1 = f32[512,128,1]{1,0,2:T(8,128)S(1)} copy-done((f32[512,128,1]{1,0,2:T(8,128)S(1)}, f32[512,128,1]{1,0,2:T(8,128)}, u32[]{:S(2)}) %copy-start.1) | copy-done | bytes 262168
  19.0 0.4 fusion
  19.4 0.6 copy-done.6
  20.0 0.3 fusion.23
  20.4 0.2 copy.71
  20.6 0.9 copy-done.3
  21.5 0.3 fusion.1
  21.8 0.7 convert_element_type.81
  22.5 3.5 %all-to-all-start.1 = ((bf16[16,10,256]{2,1,0:T(8,128)(2,1)}), bf16[16,10,256]{2,1,0:T(8,128)(2,1)S(1)}, u32[]{:S(2)}, u32[]{:S(2)}) async-start(bf16[16,10,256]{2,1,0:T(8,128)(2,1)} %convert_element_type.81), calls=%async_computation.1 | async-start | bytes 262144 | tf_op jit(solution)/shard_map/all_to_all | solution.py:101
  26.0 7.8 %all-to-all-done.1 = bf16[16,10,256]{2,1,0:T(8,128)(2,1)S(1)} async-done(((bf16[16,10,256]{2,1,0:T(8,128)(2,1)}), bf16[16,10,256]{2,1,0:T(8,128)(2,1)S(1)}, u32[]{:S(2)}, u32[]{:S(2)}) %all-to-all-start.1) | async-done | bytes 81952 | tf_op jit(solution)/shard_map/all_to_all | solution.py:101
  33.9 0.1 copy.72
  34.0 0.8 copy-done.2
  34.9 0.7 copy-done.9
  35.7 4.7 %all_gather.10 = f32[2,3,16,256]{3,2,1,0:T(8,128)S(1)} all-gather(f32[1,3,16,256]{3,2,1,0:T(8,128)S(1)} %bitcast_dynamic-update-slice_fusion), channel_id=1, replica_groups=mesh['grp'=2,'sp'=16] {'grp'}, dimensions={0}, use_global_device_ids=true | all-gather | bytes 147456 | tf_op jit(solution)/shard_map/all_gather | solution.py:107
  40.5 4.4 %collective-permute-start.1 = (f32[3,16,8]{2,1,0:T(8,128)S(1)}, f32[3,16,8]{2,1,0:T(8,128)S(1)}, u32[]{:S(2)}, u32[]{:S(2)}) collective-permute-start(f32[3,16,8]{2,1,0:T(8,128)S(1)} %get-tuple-element.34), channel_id=1, source_target_pairs={{1,0},{2,1},{3,2},{4,3},{5,4},{6,5},{7,6},{8,7},{9,8},{10,9},{11,1... | collective-permute-start | bytes 4616 | tf_op jit(solution)/shard_map/ppermute | solution.py:76
  45.0 1.5 %collective-permute-done = f32[3,16,8]{2,1,0:T(8,128)S(1)} collective-permute-done((f32[3,16,8]{2,1,0:T(8,128)S(1)}, f32[3,16,8]{2,1,0:T(8,128)S(1)}, u32[]{:S(2)}, u32[]{:S(2)}) %collective-permute-start) | collective-permute-done | bytes 1568 | tf_op jit(solution)/shard_map/ppermute | solution.py:75
  46.5 0.1 pad_maximum_fusion.2
  47.0 0.1 fusion.60
  47.4 0.4 fusion.4
  47.8 0.6 copy-done.14
  48.5 0.4 fusion.3
  48.9 4.5 %all_gather.11 = f32[3,16,256]{2,1,0:T(8,128)S(1)} all-gather(f32[3,8,256]{2,1,0:T(8,128)S(1)} %fusion.57), channel_id=1, replica_groups=mesh['grp'=2,'sp'=16] {'grp'}, dimensions={1}, use_global_device_ids=true | all-gather | bytes 73728 | tf_op jit(solution)/shard_map/all_gather | solution.py:128
  53.4 4.4 %collective-permute-start.3 = (f32[3,16,8]{2,1,0:T(8,128)S(1)}, f32[3,16,8]{2,1,0:T(8,128)S(1)}, u32[]{:S(2)}, u32[]{:S(2)}) collective-permute-start(f32[3,16,8]{2,1,0:T(8,128)S(1)} %get-tuple-element.32), channel_id=1, source_target_pairs={{1,0},{2,1},{3,2},{4,3},{5,4},{6,5},{7,6},{8,7},{9,8},{10,9},{11,1... | collective-permute-start | bytes 4616 | tf_op jit(solution)/shard_map/ppermute | solution.py:76
  58.0 1.4 %collective-permute-done.2 = f32[3,16,8]{2,1,0:T(8,128)S(1)} collective-permute-done((f32[3,16,8]{2,1,0:T(8,128)S(1)}, f32[3,16,8]{2,1,0:T(8,128)S(1)}, u32[]{:S(2)}, u32[]{:S(2)}) %collective-permute-start.2) | collective-permute-done | bytes 1568 | tf_op jit(solution)/shard_map/ppermute | solution.py:75
  59.4 0.1 pad_maximum_fusion.3
  59.7 0.1 fusion.41
  60.2 0.1 fusion.68
  60.5 13.5 %all_to_all.20 = bf16[16,10,256]{2,1,0:T(8,128)(2,1)S(1)} all-to-all(bf16[16,10,256]{2,1,0:T(8,128)(2,1)S(1)} %copy.73), channel_id=1, replica_groups=mesh['grp'=2,'sp'=16] {'sp'}, dimensions={0} | all-to-all | bytes 163840 | tf_op jit(solution)/shard_map/all_to_all | solution.py:98
  74.0 0.2 fusion.96
  74.4 0.4 convolution_multiply_fusion
  74.8 0.6 copy-done.5
  75.4 0.3 fusion.21
  75.7 0.2 copy.77
  76.0 0.3 fusion.2
  76.3 0.7 convert_element_type.96
  77.0 3.6 %all-to-all-start.3 = ((bf16[16,10,256]{2,1,0:T(8,128)(2,1)}), bf16[16,10,256]{2,1,0:T(8,128)(2,1)S(1)}, u32[]{:S(2)}, u32[]{:S(2)}) async-start(bf16[16,10,256]{2,1,0:T(8,128)(2,1)} %convert_element_type.96), calls=%async_computation.3 | async-start | bytes 262144 | tf_op jit(solution)/shard_map/all_to_all | solution.py:101
  80.6 0.6 multiply_add_fusion.4
  81.3 7.2 %all-to-all-done.3 = bf16[16,10,256]{2,1,0:T(8,128)(2,1)S(1)} async-done(((bf16[16,10,256]{2,1,0:T(8,128)(2,1)}), bf16[16,10,256]{2,1,0:T(8,128)(2,1)S(1)}, u32[]{:S(2)}, u32[]{:S(2)}) %all-to-all-start.3) | async-done | bytes 81952 | tf_op jit(solution)/shard_map/all_to_all | solution.py:101
  88.5 0.1 bitcast_add_fusion
  88.6 0.8 copy.79
  (88 shorter events, 2.8 us)
Async XLA Ops:
  2.2 7.5 %copy-start.11 = (s32[1024]{0:T(1024)S(1)}, s32[1024]{0:T(1024)}, u32[]{:S(2)}) copy-start(s32[1024]{0:T(1024)} %param.27) | copy-start | bytes 12292
  2.2 7.6 %copy-start.12 = (s32[1024]{0:T(1024)S(1)}, s32[1024]{0:T(1024)}, u32[]{:S(2)}) copy-start(s32[1024]{0:T(1024)} %param.26) | copy-start | bytes 12292
  2.3 15.4 %all-to-all-start = ((bf16[16,10,256]{2,1,0:T(8,128)(2,1)}), bf16[16,10,256]{2,1,0:T(8,128)(2,1)S(1)}, u32[]{:S(2)}, u32[]{:S(2)}) async-start(bf16[16,10,256]{2,1,0:T(8,128)(2,1)} %copy.66), calls=%async_computation | async-start | bytes 262144 | tf_op jit(solution)/shard_map/all_to_all | solution.py:98
  9.8 0.7 copy-start.7
  10.5 0.7 copy-start.8
  11.3 0.7 copy-start.13
  11.3 6.4 %copy-start = (f32[320,160]{1,0:T(8,128)S(1)}, f32[320,160]{1,0:T(8,128)}, u32[]{:S(2)}) copy-start(f32[320,160]{1,0:T(8,128)} %constant.91.clone) | copy-start | bytes 614404
  18.1 1.0 %copy-start.1 = (f32[512,128,1]{1,0,2:T(8,128)S(1)}, f32[512,128,1]{1,0,2:T(8,128)}, u32[]{:S(2)}) copy-start(f32[512,128,1]{1,0,2:T(8,128)} %constant.117) | copy-start | bytes 786436
  19.0 0.9 %copy-start.6 = (f32[2,256,128,1]{2,1,0,3:T(8,128)S(1)}, f32[2,256,128,1]{2,1,0,3:T(8,128)}, u32[]{:S(2)}) copy-start(f32[2,256,128,1]{2,1,0,3:T(8,128)} %constant.118) | copy-start | bytes 786436
  20.6 0.9 %copy-start.3 = (f32[160,320]{1,0:T(8,128)S(1)}, f32[160,320]{1,0:T(8,128)}, u32[]{:S(2)}) copy-start(f32[160,320]{1,0:T(8,128)} %constant.96.clone) | copy-start | bytes 614404
  22.5 11.4 %all-to-all-start.1 = ((bf16[16,10,256]{2,1,0:T(8,128)(2,1)}), bf16[16,10,256]{2,1,0:T(8,128)(2,1)S(1)}, u32[]{:S(2)}, u32[]{:S(2)}) async-start(bf16[16,10,256]{2,1,0:T(8,128)(2,1)} %convert_element_type.81), calls=%async_computation.1 | async-start | bytes 262144 | tf_op jit(solution)/shard_map/all_to_all | solution.py:101
  33.9 0.9 %copy-start.2 = (bf16[10,3,16,256]{3,2,1,0:T(8,128)(2,1)S(1)}, bf16[10,3,16,256]{3,2,1,0:T(8,128)(2,1)}, u32[]{:S(2)}) copy-start(bf16[10,3,16,256]{3,2,1,0:T(8,128)(2,1)} %param.22) | copy-start | bytes 737284
  34.9 0.7 copy-start.9
  34.9 0.7 copy-start.10
  40.5 6.0 %collective-permute-start = (f32[3,16,8]{2,1,0:T(8,128)S(1)}, f32[3,16,8]{2,1,0:T(8,128)S(1)}, u32[]{:S(2)}, u32[]{:S(2)}) collective-permute-start(f32[3,16,8]{2,1,0:T(8,128)S(1)} %get-tuple-element.33), channel_id=1, source_target_pairs={{0,1},{1,2},{2,3},{3,4},{4,5},{5,6},{6,7},{7,8},{8,9},{9,10},{10,1... | collective-permute-start | bytes 4616 | tf_op jit(solution)/shard_map/ppermute | solution.py:75
  40.5 6.0 %collective-permute-start.1 = (f32[3,16,8]{2,1,0:T(8,128)S(1)}, f32[3,16,8]{2,1,0:T(8,128)S(1)}, u32[]{:S(2)}, u32[]{:S(2)}) collective-permute-start(f32[3,16,8]{2,1,0:T(8,128)S(1)} %get-tuple-element.34), channel_id=1, source_target_pairs={{1,0},{2,1},{3,2},{4,3},{5,4},{6,5},{7,6},{8,7},{9,8},{10,9},{11,1... | collective-permute-start | bytes 4616 | tf_op jit(solution)/shard_map/ppermute | solution.py:76
  47.7 0.7 copy-start.14
  47.7 0.7 copy-start.15
  53.4 6.0 %collective-permute-start.2 = (f32[3,16,8]{2,1,0:T(8,128)S(1)}, f32[3,16,8]{2,1,0:T(8,128)S(1)}, u32[]{:S(2)}, u32[]{:S(2)}) collective-permute-start(f32[3,16,8]{2,1,0:T(8,128)S(1)} %get-tuple-element.31), channel_id=1, source_target_pairs={{0,1},{1,2},{2,3},{3,4},{4,5},{5,6},{6,7},{7,8},{8,9},{9,10},{10,1... | collective-permute-start | bytes 4616 | tf_op jit(solution)/shard_map/ppermute | solution.py:75
  53.4 6.0 %collective-permute-start.3 = (f32[3,16,8]{2,1,0:T(8,128)S(1)}, f32[3,16,8]{2,1,0:T(8,128)S(1)}, u32[]{:S(2)}, u32[]{:S(2)}) collective-permute-start(f32[3,16,8]{2,1,0:T(8,128)S(1)} %get-tuple-element.32), channel_id=1, source_target_pairs={{1,0},{2,1},{3,2},{4,3},{5,4},{6,5},{7,6},{8,7},{9,8},{10,9},{11,1... | collective-permute-start | bytes 4616 | tf_op jit(solution)/shard_map/ppermute | solution.py:76
  74.4 1.0 %copy-start.5 = (f32[2,256,128,1]{2,1,3,0:T(8,128)S(1)}, f32[2,256,128,1]{2,1,3,0:T(8,128)}, u32[]{:S(2)}) copy-start(f32[2,256,128,1]{2,1,3,0:T(8,128)} %constant.119) | copy-start | bytes 786436
  77.0 11.5 %copy-start.4 = (f32[10,16,256]{2,1,0:T(8,128)S(1)}, f32[10,16,256]{2,1,0:T(8,128)}, u32[]{:S(2)}) copy-start(f32[10,16,256]{2,1,0:T(8,128)} %param.21) | copy-start | bytes 491524
  77.0 11.5 %all-to-all-start.3 = ((bf16[16,10,256]{2,1,0:T(8,128)(2,1)}), bf16[16,10,256]{2,1,0:T(8,128)(2,1)S(1)}, u32[]{:S(2)}, u32[]{:S(2)}) async-start(bf16[16,10,256]{2,1,0:T(8,128)(2,1)} %convert_element_type.96), calls=%async_computation.3 | async-start | bytes 262144 | tf_op jit(solution)/shard_map/all_to_all | solution.py:101
